TPU v7x, 256 devices: a whole 4x4x8 slice. The times are simulated.
256 devices in a mesh: vec: 128 (over y, x, z), ao: 2 (over core).
Axes of the slice: x: 4, y: 4, z: 8, core: 2. Of those that a mesh axis runs over, the one named last changes fastest.
Arguments:
- cholesky: float32 [128, 1200, 1200], P('vec', 'ao'), may hold values from -6 to 6
- coefficients: float32 [2, 720000], P('ao', 'vec'), may hold values from -0.1875 to 0.1875
Outputs:
- mo_vectors: float32 [128, 128, 1072], P(None, 'vec', 'ao')
All inputs are finite; a program needn't handle non-finite values.
Results may differ from a plain program's by a relative error of at most 0.0001.
Values sent between devices are 32-bit elements; how exact they have to be, the bound alone decides.
No kernel may reach another device: no remote copies, remote signals or barrier semaphores. Data moves between devices by JAX's collectives and lax.ppermute only.
A program may use at most 64 MiB of HBM per device.

v0:
```python
import jax
import jax.numpy as jnp
from jax import lax
from jax.sharding import Mesh
from jax.sharding import PartitionSpec as P

NOCC = 128
VEC = ("vec_0", "vec_1", "vec_2")


def laid_out(blocks, dim):
    dims = list(blocks.shape[1:])
    dims[dim] *= blocks.shape[0]
    return jnp.moveaxis(blocks, 0, dim).reshape(dims)


def all_blocks(x, axes, turns):
    blocks = x
    for k in turns:
        blocks = lax.all_gather(blocks, axes[k])
    done = turns[::-1]
    back = [done.index(k) for k in range(len(axes))]
    blocks = blocks.transpose(*back, *range(len(axes), blocks.ndim))
    return blocks.reshape(-1, *x.shape)


def gathered_by_axis(x, axes, turns, dim):
    return laid_out(all_blocks(x, axes, turns), dim)


def split_up(x, dim, peers):
    dims = x.shape
    blocks = x.reshape(*dims[:dim], peers, dims[dim] // peers, *dims[dim + 1 :])
    return jnp.moveaxis(blocks, dim, 0)


def summed_on_arrival(x, axis, dim):
    blocks = split_up(x, dim, lax.axis_size(axis))
    arrived = lax.all_to_all(blocks, axis, split_axis=0, concat_axis=0, tiled=True)
    return arrived.sum(axis=0)


def body(cholesky, coefficients):
    half_rows = cholesky.shape[1]
    own_flat = gathered_by_axis(coefficients, VEC, (0, 1, 2), 1)
    own_rows = own_flat.reshape(half_rows, own_flat.shape[1] // half_rows)
    occupied_own = own_rows[:, :NOCC]
    partial_x = jnp.einsum(
        "mi,pmn->pin",
        occupied_own,
        cholesky,
        precision=lax.Precision.HIGHEST,
        preferred_element_type=jnp.float32,
    )
    x_block = lax.psum_scatter(partial_x, "ao", scatter_dimension=2, tiled=True)
    virtual_own = own_rows[:, NOCC:]
    partial_y = jnp.einsum(
        "pin,na->pia",
        x_block,
        virtual_own,
        precision=lax.Precision.HIGHEST,
        preferred_element_type=jnp.float32,
    )
    summed = summed_on_arrival(partial_y, "ao", 2)
    owned = lax.all_to_all(summed, VEC, split_axis=1, concat_axis=0, tiled=True)
    return owned


def solution(mesh):
    split = Mesh(mesh.devices.reshape(4, 4, 8, mesh.shape["ao"]), ("vec_0", "vec_1", "vec_2", "ao"))
    in_specs = (P(VEC, "ao", None), P("ao", VEC))
    out_specs = P(None, VEC, "ao")
    return jax.shard_map(body, mesh=split, in_specs=in_specs, out_specs=out_specs, check_vma=False)
```

profile of v0, /device:TPU:1, one launch (start us, length us, event | category | flops | bytes accessed | tf_op | source)
XLA Modules:
  0.0 160.1 jit_solution(18284639946833057728)
XLA Ops:
  6.5 0.0 copy-start
  6.5 0.0 all-gather.7.cloned.1.call-start
  6.5 10.8 %all-gather.3 = f32[4,1,5625]{2,1,0:T(1,128)S(1)} all-gather(f32[1,1,5625]{2,1,0:T(1,128)} %bitcast.48), channel_id=2, replica_groups=mesh['vec_0'=4,'vec_1'=4,'vec_2'=8,'ao'=2] {'vec_0'}, dimensions={0}, use_global_device_ids=true | all-gather | bytes 112500 | tf_op jit(solution)/shard_map/all_gather | solution.py:20
  17.3 10.7 %all-gather.4 = f32[4,4,5625]{2,1,0:T(4,128)} all-gather(f32[1,4,5625]{2,1,0:T(4,128)S(1)} %copy.12), channel_id=3, replica_groups=mesh['vec_0'=4,'vec_1'=4,'vec_2'=8,'ao'=2] {'vec_1'}, dimensions={0}, use_global_device_ids=true | all-gather | bytes 450000 | tf_op jit(solution)/shard_map/all_gather | solution.py:20
  28.0 0.0 all-gather.7.cloned.1.call-update
  28.0 0.0 reduce-scatter.6.cloned.1.call-start
  28.1 48.9 %all-gather.7.cloned.1.call-done = f32[32,4,1,5625]{3,1,2,0:T(4,128)} async-done(((f32[4,4,1,5625]{3,1,2,0:T(4,128)}), f32[32,4,1,5625]{3,1,2,0:T(4,128)}) %all-gather.7.cloned.1.call-update) | async-done | bytes 2880016 | tf_op jit(solution)/shard_map/all_gather | solution.py:20
  76.9 5.1 %copy.14 = f32[4,4,8,1,5625]{4,2,1,0,3:T(8,128)} copy(f32[4,4,8,1,5625]{4,0,1,2,3:T(4,128)} %bitcast.43) | data formatting | bytes 5760000 | tf_op jit(solution)/shard_map/transpose | solution.py:23
  82.0 6.5 %reshape_reshape_transpose_reshape.3 = f32[600,1200]{1,0:T(8,128)} reshape(f32[4,4,8,1,5625]{4,2,1,0,3:T(8,128)} %copy.14) | data formatting | bytes 5760000 | tf_op jit(solution)/shard_map/reshape;reshape;transpose;reshape | solution.py:46
  88.5 0.0 copy-done
  88.5 7.1 %fusion.2 = f32[1,128,1200]{1,2,0:T(8,128)} fusion(f32[1,600,1200]{2,1,0:T(8,128)S(1)} %copy-done, f32[600,1200]{1,0:T(8,128)} %reshape_reshape_transpose_reshape.3), kind=kOutput, calls=%fused_computation.3 | convolution fusion | flops 1105920000 | bytes 3801600 | tf_op jit(solution)/shard_map/mi,pmn->pin/dot_general | solution.py:48
  95.6 0.0 reduce-scatter.6.cloned.1.call-update
  95.6 3.5 %slice_bitcast_fusion = f32[1072,600]{0,1:T(8,128)} fusion(f32[600,1200]{1,0:T(8,128)} %reshape_reshape_transpose_reshape.3), kind=kLoop, calls=%fused_computation.2 | loop fusion | bytes 5145600 | tf_op jit(solution)/shard_map/pin,na->pia/dot_general | solution.py:57
  99.2 4.6 %copy.15 = f32[1072,600]{1,0:T(8,128)} copy(f32[1072,600]{0,1:T(8,128)} %slice_bitcast_fusion) | data formatting | bytes 5145600 | tf_op jit(solution)/shard_map/pin,na->pia/dot_general | solution.py:57
  103.8 6.6 %reduce-scatter.6.cloned.1.call-done = f32[1,128,600]{1,2,0:T(8,128)} async-done(((f32[1,128,1200]{1,2,0:T(8,128)}), f32[1,128,600]{1,2,0:T(8,128)}) %reduce-scatter.6.cloned.1.call-update) | async-done | bytes 307216
  110.4 4.3 %convolution_bitcast_fusion = f32[2,1,128,536]{2,3,1,0:T(8,128)S(1)} fusion(f32[2,536,600]{2,1,0:T(8,128)} %bitcast.42, f32[1,128,600]{1,2,0:T(8,128)} %reduce-scatter.6.cloned.1.call-done), kind=kOutput, calls=%fused_computation.4 | convolution fusion | flops 987955200 | bytes 3428864 | tf_op jit(solution)/shard_map/pin,na->pia/dot_general | solution.py:57
  114.7 4.6 %all_to_all.17 = f32[2,1,128,536]{2,3,1,0:T(8,128)} all-to-all(f32[2,1,128,536]{2,3,1,0:T(8,128)S(1)} %convolution_bitcast_fusion), channel_id=1, replica_groups=mesh['vec_0'=4,'vec_1'=4,'vec_2'=8,'ao'=2] {'ao'}, dimensions={0} | all-to-all | bytes 1097728 | tf_op jit(solution)/shard_map/all_to_all | solution.py:39
  119.3 1.8 %reduce_sum.11 = f32[128,536]{0,1:T(8,128)} reduce(f32[2,1,128,536]{2,3,1,0:T(8,128)} %all_to_all.17, f32[]{:T(128)} %constant.0.clone.1), dimensions={0,1}, to_apply=%region_1.0 | reduce | flops 68608 | bytes 823300 | tf_op jit(solution)/shard_map/reduce_sum | solution.py:40
  121.1 1.1 copy.17
  122.3 29.1 %all_to_all.18 = f32[1,128,536]{2,0,1:T(1,128)} all-to-all(f32[1,128,536]{2,0,1:T(1,128)S(1)} %copy.17), channel_id=1, replica_groups=mesh['vec_0'=4,'vec_1'=4,'vec_2'=8,'ao'=2] {'vec_0','vec_1','vec_2'}, dimensions={1} | all-to-all | bytes 548864 | tf_op jit(solution)/shard_map/all_to_all | solution.py:65
  151.4 1.8 %copy.18 = f32[128,1,536]{0,2,1:T(8,128)} copy(f32[128,1,536]{2,1,0:T(1,128)} %bitcast.45) | data formatting | bytes 548864 | tf_op jit(solution)/shard_map/all_to_all | solution.py:65
  (1 shorter events, 0.0 us)
Async XLA Ops:
  6.5 82.0 %copy-start = (f32[1,600,1200]{2,1,0:T(8,128)S(1)}, f32[1,600,1200]{2,1,0:T(8,128)}, u32[]{:S(2)}) copy-start(f32[1,600,1200]{2,1,0:T(8,128)} %param.2) | copy-start | bytes 8640004
  6.5 70.4 %all-gather.7.cloned.1.call-start = ((), (), s32[]{:S(2)}) async-start(), calls=%async_computation.3 | async-start | bytes 3244032 | tf_op jit(solution)/shard_map/all_gather | solution.py:20
  28.0 82.4 %reduce-scatter.6.cloned.1.call-start = ((), (), s32[]{:S(2)}) async-start(), calls=%async_computation.4 | async-start | bytes 921600
Sparse Core Ops, SparseCore 0:
  28.1 48.7 all-gather.6
  95.8 14.5 reduce-scatter.5
where the time goes:
time: 161 us; the launch traced here: 160 us
  waiting for transfers between devices  55.5 us (34%)
  blocking collectives  55.1 us (34%)
  local copies, waits for them, and re-layouts  22.7 us (14%)
  between operations  13.4 us (8%)
  matrix products  11.4 us (7%)
  other arithmetic  1.81 us (1%)
    all_gather x1, waiting for transfers between devices, all_blocks(): blocks = lax.all_gather(blocks, axes[k])  48.9 us
    all_to_all x1, blocking collectives, body(): owned = lax.all_to_all(summed, VEC, split_axis=1, concat_axis=0, tiled=True)  29.1 us
    all_gather x2, blocking collectives, all_blocks(): blocks = lax.all_gather(blocks, axes[k])  21.4 us
    dot_general x2, local copies, waits for them, and re-layouts, body(): jnp.einsum('pin,na->pia', x_block, virtual_own, precision=lax.Precision.H...  8.12 us
    dot_general x1, matrix products, body(): jnp.einsum('mi,pmn->pin', occupied_own, cholesky, precision=lax.Precision...  7.07 us
    unnamed x3, waiting for transfers between devices  6.66 us
    another operation x1, local copies, waits for them, and re-layouts, body(): own_rows = own_flat.reshape(half_rows, own_flat.shape[1] // half_rows)  6.52 us
    transpose x1, local copies, waits for them, and re-layouts, all_blocks(): blocks = blocks.transpose(*back, *range(len(axes), blocks.ndim))  5.08 us
  transfers between devices with their start and end apart: 2, of which 2 were waited for; matrix products, arithmetic and copies ran while one was open for 5% of the time, Pallas kernels for 0%

commit v1 on v0

v1 whole, which is shorter than its diff:
```python
import functools

import jax
import jax.numpy as jnp
from jax import lax
from jax.experimental import pallas as pl
from jax.experimental.pallas import tpu as pltpu
from jax.sharding import Mesh
from jax.sharding import PartitionSpec as P

VEC = ("vec_0", "vec_1", "vec_2")
LANES = 128
F32, BF16 = jnp.float32, jnp.bfloat16

NAO, NOCC, NVIR = 1200, 128, 1072
HALF = 600
HALF_PAD = 640
HALF_VIR = 536
SHARD = 5625
SHARD_ROWS = 44
SHARD_PAD = SHARD_ROWS * LANES
GROUP = 16
GROUP_ROWS = 75
BLOCKS = 11
VMEM = pl.BlockSpec(memory_space=pltpu.VMEM)


def hi_lo(x):
    hi = x.astype(BF16)
    return hi, (x - hi.astype(F32)).astype(BF16)


def prepare_kernel(chol, hi_out, lo_out):
    for h in range(2):
        part = chol[0, :, h * HALF : (h + 1) * HALF]
        part = jnp.concatenate([part, jnp.zeros((HALF, HALF_PAD - HALF), F32)], axis=1)
        part = jnp.concatenate([part, jnp.zeros((HALF_PAD - HALF, HALF_PAD), F32)], axis=0)
        hi, lo = hi_lo(part)
        hi_out[h], lo_out[h] = hi, lo


def prepare(chol):
    shape = jax.ShapeDtypeStruct((2, HALF_PAD, HALF_PAD), BF16)
    return pl.pallas_call(
        prepare_kernel,
        out_shape=(shape, shape),
        in_specs=[VMEM],
        out_specs=(VMEM, VMEM),
        cost_estimate=pl.CostEstimate(flops=20_000_000, bytes_accessed=6_000_000, transcendentals=0),
        name="prepare",
    )(chol)


def rows_kernel(raw, chol_hi, chol_lo, table, keep, send):
    lane = lax.broadcasted_iota(jnp.int32, (8, LANES), 1)
    place = lax.broadcasted_iota(jnp.int32, (8, LANES), 0) * LANES + lane

    def piece(base, shard, start):
        at = shard * SHARD_ROWS + start // LANES
        shift = start % LANES
        last = GROUP * SHARD_ROWS - 8
        if at > last:
            block = pltpu.roll(raw[pl.ds(base + last, 8), :], 8 - (at - last), 0)
        else:
            block = raw[pl.ds(base + at, 8), :]
        if shift == 0:
            return block
        turned = pltpu.roll(block, LANES - shift, 1)
        return jnp.where(lane < LANES - shift, turned, pltpu.roll(turned, 7, 0))

    def group(g, carry):
        base = pl.multiple_of(g * (GROUP * SHARD_ROWS), 8)
        for r in range(GROUP_ROWS):
            for first, column, blocks in ((0, 0, 6), (6, NOCC + HALF_VIR, 5)):
                flat = r * NAO + column
                end = flat + min(blocks * LANES, NAO - column)
                shard = flat // SHARD
                start = flat - shard * SHARD
                value = piece(base, shard, start)
                if end > (shard + 1) * SHARD:
                    other = piece(base, shard + 1, start - SHARD)
                    value = jnp.where(place < SHARD - start, value, other)
                table[pl.ds(first * HALF_PAD + g * GROUP_ROWS + r, blocks, stride=HALF_PAD), :] = value[:blocks]
        return carry

    lax.fori_loop(0, 8, group, 0)
    for j in range(BLOCKS):
        table[pl.ds(j * HALF_PAD + HALF, HALF_PAD - HALF), :] = jnp.zeros((HALF_PAD - HALF, LANES), F32)

    hi, lo = hi_lo(table[0:HALF_PAD, :].T)
    both = jnp.concatenate([hi, lo], axis=0)
    own = lax.axis_index("ao")
    for h in range(2):
        part = jnp.dot(both, chol_hi[h], preferred_element_type=F32)
        part = part[:NOCC] + part[NOCC:] + jnp.dot(hi, chol_lo[h], preferred_element_type=F32)

        @pl.when(own == h)
        def _():
            keep[...] = part

        @pl.when(own != h)
        def _():
            send[...] = part


def rows_and_first(raw, chol_hi, chol_lo):
    half = jax.ShapeDtypeStruct((NOCC, HALF_PAD), F32)
    return pl.pallas_call(
        rows_kernel,
        out_shape=(jax.ShapeDtypeStruct((BLOCKS * HALF_PAD, LANES), F32), half, half),
        in_specs=[VMEM] * 3,
        out_specs=(VMEM,) * 3,
        cost_estimate=pl.CostEstimate(flops=600_000_000, bytes_accessed=10_000_000, transcendentals=0),
        name="rows_and_first",
    )(raw, chol_hi, chol_lo)


def split_kernel(table, hi_out, lo_out):
    for j in range(1, BLOCKS):
        hi, lo = hi_lo(table[j * HALF_PAD : (j + 1) * HALF_PAD, :])
        columns = pl.ds((j - 1) * LANES, LANES)
        hi_out[:, columns] = hi
        lo_out[:, columns] = lo


def split(table):
    shape = jax.ShapeDtypeStruct((HALF_PAD, 2 * HALF_PAD), BF16)
    return pl.pallas_call(
        split_kernel,
        out_shape=(shape, shape),
        in_specs=[VMEM],
        out_specs=(VMEM, VMEM),
        cost_estimate=pl.CostEstimate(flops=20_000_000, bytes_accessed=6_000_000, transcendentals=0),
        name="split",
    )(table)


def second_kernel(kept, came, vir_hi, vir_lo, keep, send):
    hi, lo = hi_lo(kept[...] + came[...])
    both = jnp.concatenate([hi, lo], axis=0)
    own = lax.axis_index("ao")
    for h in range(2):
        columns = pl.ds(h * HALF_PAD, HALF_PAD)
        part = jnp.dot(both, vir_hi[:, columns], preferred_element_type=F32)
        part = part[:NOCC] + part[NOCC:] + jnp.dot(hi, vir_lo[:, columns], preferred_element_type=F32)

        @pl.when(own == h)
        def _():
            keep[...] = part

        @pl.when(own != h)
        def _():
            send[...] = part


def second(kept, came, vir_hi, vir_lo):
    half = jax.ShapeDtypeStruct((NOCC, HALF_PAD), F32)
    return pl.pallas_call(
        second_kernel,
        out_shape=(half, half),
        in_specs=[VMEM] * 4,
        out_specs=(VMEM,) * 2,
        cost_estimate=pl.CostEstimate(flops=600_000_000, bytes_accessed=6_000_000, transcendentals=0),
        name="second",
    )(kept, came, vir_hi, vir_lo)


def to_everyone(x, axes, peers):
    return lax.all_to_all(jnp.broadcast_to(x[None], (peers, *x.shape)), axes, 0, 0, tiled=True)


def swap(x):
    return lax.ppermute(x, "ao", [(0, 1), (1, 0)])


def body(cholesky, coefficients):
    shard = jnp.pad(coefficients[0], (0, SHARD_PAD - SHARD))
    line = to_everyone(shard, "vec_2", 8)
    raw = to_everyone(line.reshape(8 * SHARD_ROWS, LANES), ("vec_0", "vec_1"), 16)
    raw = raw.reshape(128 * SHARD_ROWS, LANES)
    chol_hi, chol_lo = prepare(cholesky)
    table, keep, send = rows_and_first(raw, chol_hi, chol_lo)
    came = swap(send)
    vir_hi, vir_lo = split(table)
    keep, send = second(keep, came, vir_hi, vir_lo)
    mine = keep + swap(send)
    owned = lax.all_to_all(mine, VEC, 0, 0, tiled=True)
    return owned[:, None, :HALF_VIR]


def solution(mesh):
    split_mesh = Mesh(mesh.devices.reshape(4, 4, 8, mesh.shape["ao"]), (*VEC, "ao"))
    in_specs = (P(VEC, "ao", None), P("ao", VEC))
    out_specs = P(None, VEC, "ao")
    return jax.shard_map(body, mesh=split_mesh, in_specs=in_specs, out_specs=out_specs, check_vma=False)
```

time: 161 us -> 117 us (0.73)
  Pallas kernels: 0 us -> 22.2 us
  waiting for transfers between devices: 55.5 us -> 34.6 us
  local copies, waits for them, and re-layouts: 22.7 us -> 5.51 us
  blocking collectives: 55.1 us -> 41.6 us
  between operations: 13.4 us -> 0.06 us
  matrix products: 11.4 us -> 0 us
  starting transfers between devices: 0.04 us -> 11 us
    all_gather x1 -> x0, waiting for transfers between devices: 48.9 us -> none  [all_blocks(): blocks = lax.all_gather(blocks, axes[k])]
    all_to_all x0 -> x1, waiting for transfers between devices: none -> 32.8 us  [to_everyone(): lax.all_to_all(jnp.broadcast_to(x[None], (peers, *x.shape)), axes, 0, 0,...]
    pallas_call x0 -> x4, Pallas kernels: none -> 22.2 us  [the longest x1 9.23 us: rows_and_first(): pl.pallas_call(rows_kernel, out_shape=(jax.ShapeDtypeStruct((BLOCKS * HAL...]
    all_gather x2 -> x0, blocking collectives: 21.4 us -> none  [all_blocks(): blocks = lax.all_gather(blocks, axes[k])]
    dot_general x2 -> x0, matrix products: 11.4 us -> none  [the longest x1 7.07 us: body(): jnp.einsum('mi,pmn->pin', occupied_own, cholesky, precision=lax.Precision...]
    dot_general x2 -> x0, local copies, waits for them, and re-layouts: 8.12 us -> none  [body(): jnp.einsum('pin,na->pia', x_block, virtual_own, precision=lax.Precision.H...]
    all_to_all x2, blocking collectives: 33.7 us -> 41.6 us  [the longest x1 24.1 us: body(): owned = lax.all_to_all(mine, VEC, 0, 0, tiled=True)]
    all_to_all x0 -> x1, starting transfers between devices: none -> 6.75 us  [to_everyone(): lax.all_to_all(jnp.broadcast_to(x[None], (peers, *x.shape)), axes, 0, 0,...]
  transfers between devices with their start and end apart: 2 -> 3, of which waited for: 2 -> 2; matrix products, arithmetic and copies ran while one was open for 5% -> 0% of each run, Pallas kernels for 0% -> 7%
where the time goes in v1:
time: 117 us
  blocking collectives  41.6 us (36%)
  waiting for transfers between devices  34.6 us (30%)
  Pallas kernels  22.2 us (19%)
  starting transfers between devices  11 us (9%)
  local copies, waits for them, and re-layouts  5.51 us (5%)
  other arithmetic  1.81 us (2%)
    all_to_all x1, waiting for transfers between devices, to_everyone(): lax.all_to_all(jnp.broadcast_to(x[None], (peers, *x.shape)), axes, 0, 0,...  32.8 us
    all_to_all x1, blocking collectives, body(): owned = lax.all_to_all(mine, VEC, 0, 0, tiled=True)  24.1 us
    all_to_all x1, blocking collectives, to_everyone(): lax.all_to_all(jnp.broadcast_to(x[None], (peers, *x.shape)), axes, 0, 0,...  17.5 us
    pallas_call x1, Pallas kernels, rows_and_first(): pl.pallas_call(rows_kernel, out_shape=(jax.ShapeDtypeStruct((BLOCKS * HAL...  9.23 us
    all_to_all x1, starting transfers between devices, to_everyone(): lax.all_to_all(jnp.broadcast_to(x[None], (peers, *x.shape)), axes, 0, 0,...  6.75 us
    pallas_call x1, Pallas kernels, split(): pl.pallas_call(split_kernel, out_shape=(shape, shape), in_specs=[VMEM], o...  4.42 us
    pallas_call x1, Pallas kernels, prepare(): pl.pallas_call(prepare_kernel, out_shape=(shape, shape), in_specs=[VMEM],...  4.28 us
    pallas_call x1, Pallas kernels, second(): pl.pallas_call(second_kernel, out_shape=(half, half), in_specs=[VMEM] * 4...  4.23 us
  transfers between devices with their start and end apart: 3, of which 2 were waited for; matrix products, arithmetic and copies ran while one was open for 0% of the time, Pallas kernels for 7%

profile of v1, /device:TPU:1, one launch (start us, length us, event | category | flops | bytes accessed | tf_op | source)
XLA Modules:
  0.0 116.7 jit_solution(4256618837479879806)
XLA Ops:
  0.0 0.8 reduce
  0.8 0.1 broadcast_in_dim.16
  0.9 17.5 %all_to_all.23 = f32[8,1,5632]{2,1,0:T(1,128)S(1)} all-to-all(f32[8,1,5632]{2,1,0:T(1,128)S(1)} %broadcast_in_dim.16), channel_id=1, replica_groups=mesh['vec_0'=4,'vec_1'=4,'vec_2'=8,'ao'=2] {'vec_2'}, dimensions={0} | all-to-all | bytes 360448 | tf_op jit(solution)/shard_map/all_to_all | solution.py:169
  18.4 1.9 %broadcast_in_dim.18 = f32[16,352,128]{2,1,0:T(8,128)} broadcast(f32[352,128]{1,0:T(8,128)S(1)} %bitcast.11), dimensions={1,2} | broadcast | bytes 3063808 | tf_op jit(solution)/shard_map/broadcast_in_dim | solution.py:169
  20.2 6.8 %all-to-all-start.1 = ((f32[16,352,128]{2,1,0:T(8,128)}), f32[16,352,128]{2,1,0:T(8,128)S(1)}, u32[]{:S(2)}, u32[]{:S(2)}) async-start(f32[16,352,128]{2,1,0:T(8,128)} %broadcast_in_dim.18), calls=%async_computation.1 | async-start | bytes 5767168 | tf_op jit(solution)/shard_map/all_to_all | solution.py:169
  27.0 4.3 %prepare.1 = (bf16[2,640,640]{2,1,0:T(8,128)(2,1)}, bf16[2,640,640]{2,1,0:T(8,128)(2,1)}) custom-call(f32[1,600,1200]{2,1,0:T(8,128)} %chol.1), custom_call_target="tpu_custom_call" | custom-call | flops 20000000 | bytes 6000000 | tf_op jit(solution)/shard_map/prepare/pallas_call | solution.py:44
  31.3 32.8 %all-to-all-done.1 = f32[16,352,128]{2,1,0:T(8,128)S(1)} async-done(((f32[16,352,128]{2,1,0:T(8,128)}), f32[16,352,128]{2,1,0:T(8,128)S(1)}, u32[]{:S(2)}, u32[]{:S(2)}) %all-to-all-start.1) | async-done | bytes 2883616 | tf_op jit(solution)/shard_map/all_to_all | solution.py:169
  64.0 0.0 copy-start
  64.1 1.6 %copy-done = f32[16,352,128]{2,1,0:T(8,128)} copy-done((f32[16,352,128]{2,1,0:T(8,128)}, f32[16,352,128]{2,1,0:T(8,128)S(1)}, u32[]{:S(2)}) %copy-start) | copy-done | bytes 2883608
  65.6 9.2 %rows_and_first.1 = (f32[7040,128]{1,0:T(8,128)}, f32[128,640]{1,0:T(8,128)}, f32[128,640]{1,0:T(8,128)}) custom-call(f32[5632,128]{1,0:T(8,128)} %bitcast.9, bf16[2,640,640]{2,1,0:T(8,128)(2,1)} %get-tuple-element.14.chol_hi, bf16[2,640,640]{2,1,0:T(8,128)(2,1)} %get-tuple-element.15.chol_lo), custom_call_target="tpu_custom_call" | custom-call | flops 600000000 | bytes 10000000 | tf_op jit(solution)/shard_map/rows_and_first/pallas_call | solution.py:108
  74.9 4.2 %collective-permute-start = (f32[128,640]{1,0:T(8,128)}, f32[128,640]{1,0:T(8,128)S(1)}, u32[]{:S(2)}, u32[]{:S(2)}) collective-permute-start(f32[128,640]{1,0:T(8,128)} %get-tuple-element.17), channel_id=1, source_target_pairs={{0,1},{1,0},{2,3},{3,2},{4,5},{5,4},{6,7},{7,6},{8,9},{9,8},{10,11... | collective-permute-start | bytes 983048 | tf_op jit(solution)/shard_map/ppermute | solution.py:173
  79.1 4.4 %split.1 = (bf16[640,1280]{1,0:T(8,128)(2,1)}, bf16[640,1280]{1,0:T(8,128)(2,1)}) custom-call(f32[7040,128]{1,0:T(8,128)} %get-tuple-element.18.table), custom_call_target="tpu_custom_call" | custom-call | flops 20000000 | bytes 6000000 | tf_op jit(solution)/shard_map/split/pallas_call | solution.py:128
  83.5 0.0 collective-permute-done.came
  83.5 0.0 copy-start.1
  83.5 0.7 copy-done.1
  84.2 4.2 %second.1 = (f32[128,640]{1,0:T(8,128)}, f32[128,640]{1,0:T(8,128)}) custom-call(f32[128,640]{1,0:T(8,128)} %get-tuple-element.16.kept, f32[128,640]{1,0:T(8,128)} %copy-done.1, bf16[640,1280]{1,0:T(8,128)(2,1)} %get-tuple-element.19.vir_hi, bf16[640,1280]{1,0:T(8,128)(2,1)} %get-tuple-element.20.vir_lo), custom_call_target="tpu_custom_call" | custom-call | flops 600000000 | bytes 6000000 | tf_op jit(solution)/shard_map/second/pallas_call | solution.py:158
  88.5 0.0 collective-permute-start.1
  88.5 1.8 %collective-permute-done.1 = f32[128,640]{1,0:T(8,128)S(1)} collective-permute-done((f32[128,640]{1,0:T(8,128)}, f32[128,640]{1,0:T(8,128)S(1)}, u32[]{:S(2)}, u32[]{:S(2)}) %collective-permute-start.1) | collective-permute-done | bytes 327712 | tf_op jit(solution)/shard_map/ppermute | solution.py:173
  90.3 1.0 add_bitcast_fusion
  91.3 0.3 copy.4
  91.7 24.1 %all_to_all.24 = f32[128,1,640]{2,1,0:T(1,128)S(1)} all-to-all(f32[128,1,640]{2,1,0:T(1,128)S(1)} %copy.4), channel_id=1, replica_groups=mesh['vec_0'=4,'vec_1'=4,'vec_2'=8,'ao'=2] {'vec_0','vec_1','vec_2'}, dimensions={0} | all-to-all | bytes 655360 | tf_op jit(solution)/shard_map/all_to_all | solution.py:187
  115.9 0.8 copy.5
  (3 shorter events, 0.1 us)
Async XLA Ops:
  20.2 43.8 %all-to-all-start.1 = ((f32[16,352,128]{2,1,0:T(8,128)}), f32[16,352,128]{2,1,0:T(8,128)S(1)}, u32[]{:S(2)}, u32[]{:S(2)}) async-start(f32[16,352,128]{2,1,0:T(8,128)} %broadcast_in_dim.18), calls=%async_computation.1 | async-start | bytes 5767168 | tf_op jit(solution)/shard_map/all_to_all | solution.py:169
  64.0 1.6 %copy-start = (f32[16,352,128]{2,1,0:T(8,128)}, f32[16,352,128]{2,1,0:T(8,128)S(1)}, u32[]{:S(2)}) copy-start(f32[16,352,128]{2,1,0:T(8,128)S(1)} %all-to-all-done.1) | copy-start | bytes 8650756
  74.9 8.6 %collective-permute-start = (f32[128,640]{1,0:T(8,128)}, f32[128,640]{1,0:T(8,128)S(1)}, u32[]{:S(2)}, u32[]{:S(2)}) collective-permute-start(f32[128,640]{1,0:T(8,128)} %get-tuple-element.17), channel_id=1, source_target_pairs={{0,1},{1,0},{2,3},{3,2},{4,5},{5,4},{6,7},{7,6},{8,9},{9,8},{10,11... | collective-permute-start | bytes 983048 | tf_op jit(solution)/shard_map/ppermute | solution.py:173
  83.5 0.7 copy-start.1
  88.5 1.8 %collective-permute-start.1 = (f32[128,640]{1,0:T(8,128)}, f32[128,640]{1,0:T(8,128)S(1)}, u32[]{:S(2)}, u32[]{:S(2)}) collective-permute-start(f32[128,640]{1,0:T(8,128)} %get-tuple-element.22), channel_id=1, source_target_pairs={{0,1},{1,0},{2,3},{3,2},{4,5},{5,4},{6,7},{7,6},{8,9},{9,8},{10,11... | collective-permute-start | bytes 983048 | tf_op jit(solution)/shard_map/ppermute | solution.py:173

commit v2 on v1

--- a/solution.py
+++ b/solution.py
@@ -30,28 +30,13 @@
     return hi, (x - hi.astype(F32)).astype(BF16)
 
 
-def prepare_kernel(chol, hi_out, lo_out):
-    for h in range(2):
-        part = chol[0, :, h * HALF : (h + 1) * HALF]
-        part = jnp.concatenate([part, jnp.zeros((HALF, HALF_PAD - HALF), F32)], axis=1)
-        part = jnp.concatenate([part, jnp.zeros((HALF_PAD - HALF, HALF_PAD), F32)], axis=0)
-        hi, lo = hi_lo(part)
-        hi_out[h], lo_out[h] = hi, lo
+def padded_half(chol, h):
+    part = chol[0, :, h * HALF : (h + 1) * HALF]
+    part = jnp.concatenate([part, jnp.zeros((HALF, HALF_PAD - HALF), F32)], axis=1)
+    return jnp.concatenate([part, jnp.zeros((HALF_PAD - HALF, HALF_PAD), F32)], axis=0)
 
 
-def prepare(chol):
-    shape = jax.ShapeDtypeStruct((2, HALF_PAD, HALF_PAD), BF16)
-    return pl.pallas_call(
-        prepare_kernel,
-        out_shape=(shape, shape),
-        in_specs=[VMEM],
-        out_specs=(VMEM, VMEM),
-        cost_estimate=pl.CostEstimate(flops=20_000_000, bytes_accessed=6_000_000, transcendentals=0),
-        name="prepare",
-    )(chol)
-
-
-def rows_kernel(raw, chol_hi, chol_lo, table, keep, send):
+def rows_kernel(raw, chol, table, keep, send):
     lane = lax.broadcasted_iota(jnp.int32, (8, LANES), 1)
     place = lax.broadcasted_iota(jnp.int32, (8, LANES), 0) * LANES + lane
 
@@ -91,8 +76,9 @@
     both = jnp.concatenate([hi, lo], axis=0)
     own = lax.axis_index("ao")
     for h in range(2):
-        part = jnp.dot(both, chol_hi[h], preferred_element_type=F32)
-        part = part[:NOCC] + part[NOCC:] + jnp.dot(hi, chol_lo[h], preferred_element_type=F32)
+        chol_hi, chol_lo = hi_lo(padded_half(chol, h))
+        part = jnp.dot(both, chol_hi, preferred_element_type=F32)
+        part = part[:NOCC] + part[NOCC:] + jnp.dot(hi, chol_lo, preferred_element_type=F32)
 
         @pl.when(own == h)
         def _():
@@ -103,16 +89,17 @@
             send[...] = part
 
 
-def rows_and_first(raw, chol_hi, chol_lo):
+def rows_and_first(raw, chol):
     half = jax.ShapeDtypeStruct((NOCC, HALF_PAD), F32)
     return pl.pallas_call(
         rows_kernel,
         out_shape=(jax.ShapeDtypeStruct((BLOCKS * HALF_PAD, LANES), F32), half, half),
-        in_specs=[VMEM] * 3,
+        in_specs=[VMEM] * 2,
         out_specs=(VMEM,) * 3,
         cost_estimate=pl.CostEstimate(flops=600_000_000, bytes_accessed=10_000_000, transcendentals=0),
+        compiler_params=pltpu.CompilerParams(vmem_limit_bytes=20 * 2**20),
         name="rows_and_first",
-    )(raw, chol_hi, chol_lo)
+    )(raw, chol)
 
 
 def split_kernel(table, hi_out, lo_out):
@@ -131,6 +118,7 @@
         in_specs=[VMEM],
         out_specs=(VMEM, VMEM),
         cost_estimate=pl.CostEstimate(flops=20_000_000, bytes_accessed=6_000_000, transcendentals=0),
+        compiler_params=pltpu.CompilerParams(vmem_limit_bytes=12 * 2**20),
         name="split",
     )(table)
 
@@ -161,6 +149,7 @@
         in_specs=[VMEM] * 4,
         out_specs=(VMEM,) * 2,
         cost_estimate=pl.CostEstimate(flops=600_000_000, bytes_accessed=6_000_000, transcendentals=0),
+        compiler_params=pltpu.CompilerParams(vmem_limit_bytes=12 * 2**20),
         name="second",
     )(kept, came, vir_hi, vir_lo)
 
@@ -178,8 +167,7 @@
     line = to_everyone(shard, "vec_2", 8)
     raw = to_everyone(line.reshape(8 * SHARD_ROWS, LANES), ("vec_0", "vec_1"), 16)
     raw = raw.reshape(128 * SHARD_ROWS, LANES)
-    chol_hi, chol_lo = prepare(cholesky)
-    table, keep, send = rows_and_first(raw, chol_hi, chol_lo)
+    table, keep, send = rows_and_first(raw, cholesky)
     came = swap(send)
     vir_hi, vir_lo = split(table)
     keep, send = second(keep, came, vir_hi, vir_lo)

time: 117 us -> 95.3 us (0.81)
  blocking collectives: 41.6 us -> 79.9 us
  waiting for transfers between devices: 34.6 us -> 1.81 us
  Pallas kernels: 22.2 us -> 6.72 us
  starting transfers between devices: 11 us -> 4.07 us
  local copies, waits for them, and re-layouts: 5.51 us -> 1.61 us
    all_to_all x1 -> x2, blocking collectives: 17.5 us -> 58.7 us  [to_everyone(): lax.all_to_all(jnp.broadcast_to(x[None], (peers, *x.shape)), axes, 0, 0,...]
    all_to_all x1 -> x0, waiting for transfers between devices: 32.8 us -> none  [to_everyone(): lax.all_to_all(jnp.broadcast_to(x[None], (peers, *x.shape)), axes, 0, 0,...]
    all_to_all x1 -> x0, starting transfers between devices: 6.75 us -> none  [to_everyone(): lax.all_to_all(jnp.broadcast_to(x[None], (peers, *x.shape)), axes, 0, 0,...]
    pallas_call x1, Pallas kernels: 9.23 us -> 4.73 us  [rows_and_first(): pl.pallas_call(rows_kernel, out_shape=(jax.ShapeDtypeStruct((BLOCKS * HAL...]
    pallas_call x1 -> x0, Pallas kernels: 4.28 us -> none  [prepare(): pl.pallas_call(prepare_kernel, out_shape=(shape, shape), in_specs=[VMEM],...]
    pallas_call x1, Pallas kernels: 4.42 us -> 0.7 us  [split(): pl.pallas_call(split_kernel, out_shape=(shape, shape), in_specs=[VMEM], o...]
    all_to_all x1, blocking collectives: 24.1 us -> 21.2 us  [body(): owned = lax.all_to_all(mine, VEC, 0, 0, tiled=True)]
    pallas_call x1, Pallas kernels: 4.23 us -> 1.29 us  [second(): pl.pallas_call(second_kernel, out_shape=(half, half), in_specs=[VMEM] * 4...]
  transfers between devices with their start and end apart: 3 -> 2, of which waited for: 2 -> 2; matrix products, arithmetic and copies ran while one was open for 0% -> 0% of each run, Pallas kernels for 7% -> 1%
where the time goes in v2:
time: 95.3 us; the launch traced here: 95 us
  blocking collectives  79.9 us (84%)
  Pallas kernels  6.72 us (7%)
  starting transfers between devices  4.07 us (4%)
  waiting for transfers between devices  1.81 us (2%)
  local copies, waits for them, and re-layouts  1.61 us (2%)
    all_to_all x2, blocking collectives, to_everyone(): lax.all_to_all(jnp.broadcast_to(x[None], (peers, *x.shape)), axes, 0, 0,...  58.7 us
    all_to_all x1, blocking collectives, body(): owned = lax.all_to_all(mine, VEC, 0, 0, tiled=True)  21.2 us
    pallas_call x1, Pallas kernels, rows_and_first(): pl.pallas_call(rows_kernel, out_shape=(jax.ShapeDtypeStruct((BLOCKS * HAL...  4.73 us
    ppermute x2, starting transfers between devices, swap(): return lax.ppermute(x, 'ao', [(0, 1), (1, 0)])  4.07 us
  transfers between devices with their start and end apart: 2, of which 2 were waited for; matrix products, arithmetic and copies ran while one was open for 0% of the time, Pallas kernels for 1%

profile of v2, /device:TPU:1, one launch (start us, length us, event | category | flops | bytes accessed | tf_op | source)
XLA Modules:
  0.0 95.0 jit_solution(555062838189036172)
XLA Ops:
  0.0 0.8 reduce
  0.8 0.1 broadcast_in_dim.16
  0.9 17.5 %all_to_all.23 = f32[8,1,5632]{2,1,0:T(1,128)S(1)} all-to-all(f32[8,1,5632]{2,1,0:T(1,128)S(1)} %broadcast_in_dim.16), channel_id=1, replica_groups=mesh['vec_0'=4,'vec_1'=4,'vec_2'=8,'ao'=2] {'vec_2'}, dimensions={0} | all-to-all | bytes 360448 | tf_op jit(solution)/shard_map/all_to_all | solution.py:158
  18.4 0.3 broadcast_in_dim.18
  18.6 0.0 copy-start
  18.7 41.3 %all_to_all.24 = f32[16,352,128]{2,1,0:T(8,128)S(1)} all-to-all(f32[16,352,128]{2,1,0:T(8,128)S(1)} %broadcast_in_dim.18), channel_id=1, replica_groups=mesh['vec_0'=4,'vec_1'=4,'vec_2'=8,'ao'=2] {'vec_0','vec_1'}, dimensions={0} | all-to-all | bytes 5767168 | tf_op jit(solution)/shard_map/all_to_all | solution.py:158
  59.9 0.0 copy-done
  59.9 4.7 %rows_and_first.1 = (f32[7040,128]{1,0:T(8,128)S(1)}, f32[128,640]{1,0:T(8,128)S(1)}, f32[128,640]{1,0:T(8,128)S(1)}) custom-call(f32[5632,128]{1,0:T(8,128)S(1)} %bitcast.9, f32[1,600,1200]{2,1,0:T(8,128)S(1)} %copy-done), custom_call_target="tpu_custom_call" | custom-call | flops 600000000 | bytes 10000000 | tf_op jit(solution)/shard_map/rows_and_first/pallas_call | solution.py:94
  64.7 3.6 %collective-permute-start = (f32[128,640]{1,0:T(8,128)S(1)}, f32[128,640]{1,0:T(8,128)S(1)}, u32[]{:S(2)}, u32[]{:S(2)}) collective-permute-start(f32[128,640]{1,0:T(8,128)S(1)} %get-tuple-element.13), channel_id=1, source_target_pairs={{0,1},{1,0},{2,3},{3,2},{4,5},{5,4},{6,7},{7,6},{8,9},{9,8},{10,11... | collective-permute-start | bytes 983048 | tf_op jit(solution)/shard_map/ppermute | solution.py:162
  68.3 0.7 split.1
  69.0 0.6 collective-permute-done.came
  69.6 1.3 %second.1 = (f32[128,640]{1,0:T(8,128)S(1)}, f32[128,640]{1,0:T(8,128)S(1)}) custom-call(f32[128,640]{1,0:T(8,128)S(1)} %get-tuple-element.12.kept, f32[128,640]{1,0:T(8,128)S(1)} %collective-permute-done.came, bf16[640,1280]{1,0:T(8,128)(2,1)S(1)} %get-tuple-element.15.vir_hi, bf16[640,1280]{1,0:T(8,128)(2,1)S(1)} %get-tuple-element.16.vir_lo), custom_call_target="tpu_custom_call" | custom-call | flops 600000000 | bytes 6000000 | tf_op jit(solution)/shard_map/second/pallas_call | solution.py:146
  70.8 0.5 collective-permute-start.1
  71.3 1.3 %collective-permute-done.1 = f32[128,640]{1,0:T(8,128)S(1)} collective-permute-done((f32[128,640]{1,0:T(8,128)S(1)}, f32[128,640]{1,0:T(8,128)S(1)}, u32[]{:S(2)}, u32[]{:S(2)}) %collective-permute-start.1) | collective-permute-done | bytes 327712 | tf_op jit(solution)/shard_map/ppermute | solution.py:162
  72.6 0.3 copy.4
  72.9 21.2 %all_to_all.25 = f32[128,1,640]{2,1,0:T(1,128)S(1)} all-to-all(f32[128,1,640]{2,1,0:T(1,128)S(1)} %copy.4), channel_id=1, replica_groups=mesh['vec_0'=4,'vec_1'=4,'vec_2'=8,'ao'=2] {'vec_0','vec_1','vec_2'}, dimensions={0} | all-to-all | bytes 655360 | tf_op jit(solution)/shard_map/all_to_all | solution.py:175
  94.2 0.8 copy.5
  (4 shorter events, 0.1 us)
Async XLA Ops:
  18.6 41.3 %copy-start = (f32[1,600,1200]{2,1,0:T(8,128)S(1)}, f32[1,600,1200]{2,1,0:T(8,128)}, u32[]{:S(2)}) copy-start(f32[1,600,1200]{2,1,0:T(8,128)} %chol.1) | copy-start | bytes 8640004
  64.7 4.9 %collective-permute-start = (f32[128,640]{1,0:T(8,128)S(1)}, f32[128,640]{1,0:T(8,128)S(1)}, u32[]{:S(2)}, u32[]{:S(2)}) collective-permute-start(f32[128,640]{1,0:T(8,128)S(1)} %get-tuple-element.13), channel_id=1, source_target_pairs={{0,1},{1,0},{2,3},{3,2},{4,5},{5,4},{6,7},{7,6},{8,9},{9,8},{10,11... | collective-permute-start | bytes 983048 | tf_op jit(solution)/shard_map/ppermute | solution.py:162
  70.8 1.7 %collective-permute-start.1 = (f32[128,640]{1,0:T(8,128)S(1)}, f32[128,640]{1,0:T(8,128)S(1)}, u32[]{:S(2)}, u32[]{:S(2)}) collective-permute-start(f32[128,640]{1,0:T(8,128)S(1)} %get-tuple-element.18), channel_id=1, source_target_pairs={{0,1},{1,0},{2,3},{3,2},{4,5},{5,4},{6,7},{7,6},{8,9},{9,8},{10,11... | collective-permute-start | bytes 983048 | tf_op jit(solution)/shard_map/ppermute | solution.py:162

commit v3 on v2

--- a/solution.py
+++ b/solution.py
@@ -21,8 +21,21 @@
 SHARD_PAD = SHARD_ROWS * LANES
 GROUP = 16
 GROUP_ROWS = 75
+PITCH = HALF_PAD + 1
+LINE = 8
+LINE_ROWS = LINE * SHARD_ROWS
 BLOCKS = 11
 VMEM = pl.BlockSpec(memory_space=pltpu.VMEM)
+
+
+def plane_groups(swapped):
+    lines = []
+    for core in range(2):
+        along_0 = (core == 0) != swapped
+        for fixed in range(4):
+            cells = [(k, fixed) if along_0 else (fixed, k) for k in range(4)]
+            lines.append([(a * 4 + b) * 2 + core for a, b in cells])
+    return lines
 
 
 def hi_lo(x):
@@ -37,13 +50,15 @@
 
 
 def rows_kernel(raw, chol, table, keep, send):
+    own = lax.axis_index("ao")
     lane = lax.broadcasted_iota(jnp.int32, (8, LANES), 1)
     place = lax.broadcasted_iota(jnp.int32, (8, LANES), 0) * LANES + lane
 
-    def piece(base, shard, start):
-        at = shard * SHARD_ROWS + start // LANES
+    def piece(bases, shard, start):
+        base = bases[shard // LINE]
+        at = shard % LINE * SHARD_ROWS + start // LANES
         shift = start % LANES
-        last = GROUP * SHARD_ROWS - 8
+        last = LINE_ROWS - 8
         if at > last:
             block = pltpu.roll(raw[pl.ds(base + last, 8), :], 8 - (at - last), 0)
         else:
@@ -54,27 +69,28 @@
         return jnp.where(lane < LANES - shift, turned, pltpu.roll(turned, 7, 0))
 
     def group(g, carry):
-        base = pl.multiple_of(g * (GROUP * SHARD_ROWS), 8)
+        y, x = g // 2, g % 2 * 2
+        place_of = [jnp.where(own == 0, (x + k) * 4 + y, y * 4 + x + k) for k in range(2)]
+        bases = [pl.multiple_of(at * LINE_ROWS, 8) for at in place_of]
         for r in range(GROUP_ROWS):
             for first, column, blocks in ((0, 0, 6), (6, NOCC + HALF_VIR, 5)):
                 flat = r * NAO + column
                 end = flat + min(blocks * LANES, NAO - column)
                 shard = flat // SHARD
                 start = flat - shard * SHARD
-                value = piece(base, shard, start)
+                value = piece(bases, shard, start)
                 if end > (shard + 1) * SHARD:
-                    other = piece(base, shard + 1, start - SHARD)
+                    other = piece(bases, shard + 1, start - SHARD)
                     value = jnp.where(place < SHARD - start, value, other)
-                table[pl.ds(first * HALF_PAD + g * GROUP_ROWS + r, blocks, stride=HALF_PAD), :] = value[:blocks]
+                table[pl.ds(first * PITCH + g * GROUP_ROWS + r, blocks, stride=PITCH), :] = value[:blocks]
         return carry
 
     lax.fori_loop(0, 8, group, 0)
     for j in range(BLOCKS):
-        table[pl.ds(j * HALF_PAD + HALF, HALF_PAD - HALF), :] = jnp.zeros((HALF_PAD - HALF, LANES), F32)
+        table[pl.ds(j * PITCH + HALF, HALF_PAD - HALF), :] = jnp.zeros((HALF_PAD - HALF, LANES), F32)
 
     hi, lo = hi_lo(table[0:HALF_PAD, :].T)
     both = jnp.concatenate([hi, lo], axis=0)
-    own = lax.axis_index("ao")
     for h in range(2):
         chol_hi, chol_lo = hi_lo(padded_half(chol, h))
         part = jnp.dot(both, chol_hi, preferred_element_type=F32)
@@ -93,7 +109,7 @@
     half = jax.ShapeDtypeStruct((NOCC, HALF_PAD), F32)
     return pl.pallas_call(
         rows_kernel,
-        out_shape=(jax.ShapeDtypeStruct((BLOCKS * HALF_PAD, LANES), F32), half, half),
+        out_shape=(jax.ShapeDtypeStruct((BLOCKS * PITCH, LANES), F32), half, half),
         in_specs=[VMEM] * 2,
         out_specs=(VMEM,) * 3,
         cost_estimate=pl.CostEstimate(flops=600_000_000, bytes_accessed=10_000_000, transcendentals=0),
@@ -104,7 +120,7 @@
 
 def split_kernel(table, hi_out, lo_out):
     for j in range(1, BLOCKS):
-        hi, lo = hi_lo(table[j * HALF_PAD : (j + 1) * HALF_PAD, :])
+        hi, lo = hi_lo(table[j * PITCH : j * PITCH + HALF_PAD, :])
         columns = pl.ds((j - 1) * LANES, LANES)
         hi_out[:, columns] = hi
         lo_out[:, columns] = lo
@@ -154,8 +170,9 @@
     )(kept, came, vir_hi, vir_lo)
 
 
-def to_everyone(x, axes, peers):
-    return lax.all_to_all(jnp.broadcast_to(x[None], (peers, *x.shape)), axes, 0, 0, tiled=True)
+def to_everyone(x, axes, peers, groups=None):
+    copies = jnp.broadcast_to(x[None], (peers, *x.shape)).reshape(-1, x.shape[-1])
+    return lax.all_to_all(copies, axes, 0, 0, tiled=True, axis_index_groups=groups)
 
 
 def swap(x):
@@ -163,9 +180,11 @@
 
 
 def body(cholesky, coefficients):
-    shard = jnp.pad(coefficients[0], (0, SHARD_PAD - SHARD))
-    line = to_everyone(shard, "vec_2", 8)
-    raw = to_everyone(line.reshape(8 * SHARD_ROWS, LANES), ("vec_0", "vec_1"), 16)
+    shard = jnp.pad(coefficients, ((0, 0), (0, SHARD_PAD - SHARD)))
+    line = to_everyone(shard, "vec_2", LINE)
+    plane = ("vec_0", "vec_1", "ao")
+    raw = to_everyone(line.reshape(LINE_ROWS, LANES), plane, 4, plane_groups(False))
+    raw = to_everyone(raw.reshape(4 * LINE_ROWS, LANES), plane, 4, plane_groups(True))
     raw = raw.reshape(128 * SHARD_ROWS, LANES)
     table, keep, send = rows_and_first(raw, cholesky)
     came = swap(send)

time: 95.3 us -> 90.1 us (0.945)
  blocking collectives: 79.9 us -> 74.2 us
  starting transfers between devices: 4.07 us -> 5.83 us
  Pallas kernels: 6.72 us -> 5.56 us
    all_to_all x2 -> x3, blocking collectives: 58.7 us -> 53.1 us  [to_everyone(): lax.all_to_all(copies, axes, 0, 0, tiled=True, axis_index_groups=groups)]
    ppermute x2, starting transfers between devices: 4.07 us -> 5.83 us  [swap(): return lax.ppermute(x, 'ao', [(0, 1), (1, 0)])]
    pallas_call x1, Pallas kernels: 4.73 us -> 3.58 us  [rows_and_first(): pl.pallas_call(rows_kernel, out_shape=(jax.ShapeDtypeStruct((BLOCKS * PIT...]
where the time goes in v3:
time: 90.1 us; the launch traced here: 89.8 us
  blocking collectives  74.2 us (82%)
  starting transfers between devices  5.83 us (6%)
  Pallas kernels  5.56 us (6%)
  local copies, waits for them, and re-layouts  2.36 us (3%)
  waiting for transfers between devices  1.81 us (2%)
    all_to_all x3, blocking collectives, to_everyone(): lax.all_to_all(copies, axes, 0, 0, tiled=True, axis_index_groups=groups)  53.1 us
    all_to_all x1, blocking collectives, body(): owned = lax.all_to_all(mine, VEC, 0, 0, tiled=True)  21.1 us
    ppermute x2, starting transfers between devices, swap(): return lax.ppermute(x, 'ao', [(0, 1), (1, 0)])  5.83 us
    pallas_call x1, Pallas kernels, rows_and_first(): pl.pallas_call(rows_kernel, out_shape=(jax.ShapeDtypeStruct((BLOCKS * PIT...  3.58 us
    ppermute x2, waiting for transfers between devices, swap(): return lax.ppermute(x, 'ao', [(0, 1), (1, 0)])  1.81 us
  transfers between devices with their start and end apart: 2, of which 2 were waited for; matrix products, arithmetic and copies ran while one was open for 0% of the time, Pallas kernels for 1%

profile of v3, /device:TPU:1, one launch (start us, length us, event | category | flops | bytes accessed | tf_op | source)
XLA Modules:
  0.0 89.8 jit_solution(8863417247188894166)
XLA Ops:
  0.0 0.8 pad_reduce_fusion
  0.8 0.1 reshape.26
  0.9 17.5 %all_to_all.32 = f32[8,1,5632]{2,1,0:T(1,128)S(1)} all-to-all(f32[8,1,5632]{2,1,0:T(1,128)S(1)} %reshape.26), channel_id=1, replica_groups=mesh['vec_0'=4,'vec_1'=4,'vec_2'=8,'ao'=2] {'vec_2'}, dimensions={0} | all-to-all | bytes 360448 | tf_op jit(solution)/shard_map/all_to_all | solution.py:175
  18.4 12.1 %all_to_all.33 = f32[4,352,128]{2,1,0:T(8,128)S(1)} all-to-all(f32[4,352,128]{2,1,0:T(8,128)S(1)} %broadcast_in_dim.11), channel_id=1, replica_groups={{0,64,128,192},{16,80,144,208},{32,96,160,224},{48,112,176,240},{1,17,3..., dimensions={0} | all-to-all | bytes 1441792 | tf_op jit(solution)/shard_map/all_to_all | solution.py:175
  30.5 0.2 broadcast_in_dim.25
  30.7 0.0 copy-start
  30.7 23.5 %all_to_all.34 = f32[4,1408,128]{2,1,0:T(8,128)S(1)} all-to-all(f32[4,1408,128]{2,1,0:T(8,128)S(1)} %broadcast_in_dim.25), channel_id=1, replica_groups={{0,16,32,48},{64,80,96,112},{128,144,160,176},{192,208,224,240},{1,65,1..., dimensions={0} | all-to-all | bytes 5767168 | tf_op jit(solution)/shard_map/all_to_all | solution.py:175
  54.2 0.0 copy-done
  54.2 3.6 %rows_and_first.1 = (f32[7051,128]{1,0:T(8,128)S(1)}, f32[128,640]{1,0:T(8,128)S(1)}, f32[128,640]{1,0:T(8,128)S(1)}) custom-call(f32[5632,128]{1,0:T(8,128)S(1)} %bitcast.10, f32[1,600,1200]{2,1,0:T(8,128)S(1)} %copy-done), custom_call_target="tpu_custom_call" | custom-call | flops 600000000 | bytes 10000000 | tf_op jit(solution)/shard_map/rows_and_first/pallas_call | solution.py:110
  57.8 5.4 %collective-permute-start = (f32[128,640]{1,0:T(8,128)S(1)}, f32[128,640]{1,0:T(8,128)S(1)}, u32[]{:S(2)}, u32[]{:S(2)}) collective-permute-start(f32[128,640]{1,0:T(8,128)S(1)} %get-tuple-element.13), channel_id=1, source_target_pairs={{0,1},{1,0},{2,3},{3,2},{4,5},{5,4},{6,7},{7,6},{8,9},{9,8},{10,11... | collective-permute-start | bytes 983048 | tf_op jit(solution)/shard_map/ppermute | solution.py:179
  63.2 0.7 split.1
  63.9 0.6 collective-permute-done.came
  64.4 1.3 %second.1 = (f32[128,640]{1,0:T(8,128)S(1)}, f32[128,640]{1,0:T(8,128)S(1)}) custom-call(f32[128,640]{1,0:T(8,128)S(1)} %get-tuple-element.12.kept, f32[128,640]{1,0:T(8,128)S(1)} %collective-permute-done.came, bf16[640,1280]{1,0:T(8,128)(2,1)S(1)} %get-tuple-element.15.vir_hi, bf16[640,1280]{1,0:T(8,128)(2,1)S(1)} %get-tuple-element.16.vir_lo), custom_call_target="tpu_custom_call" | custom-call | flops 600000000 | bytes 6000000 | tf_op jit(solution)/shard_map/second/pallas_call | solution.py:162
  65.7 0.5 collective-permute-start.1
  66.2 1.3 %collective-permute-done.1 = f32[128,640]{1,0:T(8,128)S(1)} collective-permute-done((f32[128,640]{1,0:T(8,128)S(1)}, f32[128,640]{1,0:T(8,128)S(1)}, u32[]{:S(2)}, u32[]{:S(2)}) %collective-permute-start.1) | collective-permute-done | bytes 327712 | tf_op jit(solution)/shard_map/ppermute | solution.py:179
  67.5 0.3 copy.4
  67.8 21.1 %all_to_all.35 = f32[128,1,640]{2,1,0:T(1,128)S(1)} all-to-all(f32[128,1,640]{2,1,0:T(1,128)S(1)} %copy.4), channel_id=1, replica_groups=mesh['vec_0'=4,'vec_1'=4,'vec_2'=8,'ao'=2] {'vec_0','vec_1','vec_2'}, dimensions={0} | all-to-all | bytes 655360 | tf_op jit(solution)/shard_map/all_to_all | solution.py:194
  89.0 0.8 copy.5
  (4 shorter events, 0.1 us)
Async XLA Ops:
  30.7 23.5 %copy-start = (f32[1,600,1200]{2,1,0:T(8,128)S(1)}, f32[1,600,1200]{2,1,0:T(8,128)}, u32[]{:S(2)}) copy-start(f32[1,600,1200]{2,1,0:T(8,128)} %chol.1) | copy-start | bytes 8640004
  57.8 6.6 %collective-permute-start = (f32[128,640]{1,0:T(8,128)S(1)}, f32[128,640]{1,0:T(8,128)S(1)}, u32[]{:S(2)}, u32[]{:S(2)}) collective-permute-start(f32[128,640]{1,0:T(8,128)S(1)} %get-tuple-element.13), channel_id=1, source_target_pairs={{0,1},{1,0},{2,3},{3,2},{4,5},{5,4},{6,7},{7,6},{8,9},{9,8},{10,11... | collective-permute-start | bytes 983048 | tf_op jit(solution)/shard_map/ppermute | solution.py:179
  65.7 1.7 %collective-permute-start.1 = (f32[128,640]{1,0:T(8,128)S(1)}, f32[128,640]{1,0:T(8,128)S(1)}, u32[]{:S(2)}, u32[]{:S(2)}) collective-permute-start(f32[128,640]{1,0:T(8,128)S(1)} %get-tuple-element.18), channel_id=1, source_target_pairs={{0,1},{1,0},{2,3},{3,2},{4,5},{5,4},{6,7},{7,6},{8,9},{9,8},{10,11... | collective-permute-start | bytes 983048 | tf_op jit(solution)/shard_map/ppermute | solution.py:179

commit v4 on v3

v4 whole, which is shorter than its diff:
```python
import functools

import jax
import jax.numpy as jnp
from jax import lax
from jax.experimental import pallas as pl
from jax.experimental.pallas import tpu as pltpu
from jax.sharding import Mesh
from jax.sharding import PartitionSpec as P

VEC = ("vec_0", "vec_1", "vec_2")
LANES = 128
F32, BF16 = jnp.float32, jnp.bfloat16

NAO, NOCC, NVIR = 1200, 128, 1072
HALF = 600
HALF_PAD = 640
HALF_VIR = 536
SHARD = 5625
SHARD_ROWS = 44
SHARD_PAD = SHARD_ROWS * LANES
GROUP = 16
GROUP_ROWS = 75
PITCH = HALF_PAD + 1
LINE = 8
LINE_ROWS = LINE * SHARD_ROWS
HALF_BLOCKS = 5
VMEM = pl.BlockSpec(memory_space=pltpu.VMEM)


def plane_groups(swapped):
    lines = []
    for core in range(2):
        along_0 = (core == 0) != swapped
        for fixed in range(4):
            cells = [(k, fixed) if along_0 else (fixed, k) for k in range(4)]
            lines.append([(a * 4 + b) * 2 + core for a, b in cells])
    return lines


def hi_lo(x):
    hi = x.astype(BF16)
    return hi, (x - hi.astype(F32)).astype(BF16)


def padded_half(chol, h):
    part = chol[0, :, h * HALF : (h + 1) * HALF]
    part = jnp.concatenate([part, jnp.zeros((HALF, HALF_PAD - HALF), F32)], axis=1)
    return jnp.concatenate([part, jnp.zeros((HALF_PAD - HALF, HALF_PAD), F32)], axis=0)


def each_row(raw, column, columns, store):
    own = lax.axis_index("ao")
    lane = lax.broadcasted_iota(jnp.int32, (8, LANES), 1)
    place = lax.broadcasted_iota(jnp.int32, (8, LANES), 0) * LANES + lane

    def piece(bases, shard, start):
        base = bases[shard // LINE]
        at = shard % LINE * SHARD_ROWS + start // LANES
        shift = start % LANES
        last = LINE_ROWS - 8
        if at > last:
            block = pltpu.roll(raw[pl.ds(base + last, 8), :], 8 - (at - last), 0)
        else:
            block = raw[pl.ds(base + at, 8), :]
        if shift == 0:
            return block
        turned = pltpu.roll(block, LANES - shift, 1)
        return jnp.where(lane < LANES - shift, turned, pltpu.roll(turned, 7, 0))

    def group(g, carry):
        y, x = g // 2, g % 2 * 2
        place_of = [jnp.where(own == 0, (x + k) * 4 + y, y * 4 + x + k) for k in range(2)]
        bases = [pl.multiple_of(at * LINE_ROWS, 8) for at in place_of]
        for r in range(GROUP_ROWS):
            flat = r * NAO + column
            shard = flat // SHARD
            start = flat - shard * SHARD
            value = piece(bases, shard, start)
            if start + columns > SHARD:
                other = piece(bases, shard + 1, start - SHARD)
                value = jnp.where(place < SHARD - start, value, other)
            store(g * GROUP_ROWS + r, value)
        return carry

    lax.fori_loop(0, 8, group, 0)


def three_products(both, hi, lo):
    part = jnp.dot(both, hi, preferred_element_type=F32)
    return part[:NOCC] + part[NOCC:] + jnp.dot(both[:NOCC], lo, preferred_element_type=F32)


def for_half(mine, out, compute):
    own = lax.axis_index("ao")
    for h in range(2):

        @pl.when((own == h) if mine else (own != h))
        def _():
            out[...] = compute(h)


def first_half(both, chol, h):
    return three_products(both, *hi_lo(padded_half(chol, h)))


def occupied_rows(raw, occupied, core):
    lane = lax.broadcasted_iota(jnp.int32, (8, LANES), 1)

    def lines(line, at):
        parts = []
        for h in range(2):
            start, stride = ((2 * h + line) * 4, 1) if core == 0 else (2 * h + line, 4)
            parts.append(raw[pl.ds(start * LINE_ROWS + at, 4, stride=stride * LINE_ROWS), :])
        return jnp.concatenate(parts, axis=0)

    def piece(shard, start):
        at = shard % LINE * SHARD_ROWS + start // LANES
        shift = start % LANES
        rows = [lines(shard // LINE, min(max(q, 0), LINE_ROWS - 1)) for q in (at, at + 1)]
        if shift == 0:
            return rows[0]
        low, high = (pltpu.roll(q, LANES - shift, 1) for q in rows)
        return jnp.where(lane < LANES - shift, low, high)

    for r in range(GROUP_ROWS):
        shard = r * NAO // SHARD
        start = r * NAO - shard * SHARD
        value = piece(shard, start)
        if start + NOCC > SHARD:
            value = jnp.where(lane < SHARD - start, value, piece(shard + 1, start - SHARD))
        for h in range(2):
            occupied[pl.ds(h * GROUP_ROWS + r, 4, stride=2 * GROUP_ROWS), :] = value[4 * h : 4 * h + 4]


def occupied_kernel(raw, chol, both_out, send, occupied):
    own = lax.axis_index("ao")
    for core in range(2):

        @pl.when(own == core)
        def _():
            occupied_rows(raw, occupied, core)

    occupied[HALF:, :] = jnp.zeros((HALF_PAD - HALF, LANES), F32)
    both = jnp.concatenate(hi_lo(occupied[...].T), axis=0)
    both_out[...] = both
    for_half(False, send, lambda h: first_half(both, chol, h))


def virtual_rows(raw, table, mine):
    own = lax.axis_index("ao")

    def store(row, value):
        table[pl.ds(row, HALF_BLOCKS, stride=PITCH), :] = value[:HALF_BLOCKS]

    for h in range(2):

        @pl.when((own == h) if mine else (own != h))
        def _():
            each_row(raw, NOCC + h * HALF_VIR, HALF_VIR, store)

    for j in range(HALF_BLOCKS):
        table[pl.ds(j * PITCH + HALF, PITCH - HALF), :] = jnp.zeros((PITCH - HALF, LANES), F32)


def second_half(both, table):
    blocks = [table[j * PITCH : j * PITCH + HALF_PAD, :] for j in range(HALF_BLOCKS)]
    return three_products(both, *hi_lo(jnp.concatenate(blocks, axis=1)))


def middle_kernel(raw, chol, both, table, keep):
    virtual_rows(raw, table, False)
    for_half(True, keep, lambda h: first_half(both[...], chol, h))


def leaving_kernel(kept, came, table, both_out, send):
    both = jnp.concatenate(hi_lo(kept[...] + came[...]), axis=0)
    both_out[...] = both
    send[...] = second_half(both, table)


def staying_kernel(raw, both, keep, table):
    virtual_rows(raw, table, True)
    keep[...] = second_half(both[...], table)


def call(kernel, outs, *args, scratch=(), mib=16):
    return pl.pallas_call(
        kernel,
        out_shape=outs,
        in_specs=[VMEM] * len(args),
        out_specs=(VMEM,) * len(outs),
        scratch_shapes=scratch,
        compiler_params=pltpu.CompilerParams(vmem_limit_bytes=mib * 2**20),
        cost_estimate=pl.CostEstimate(flops=600_000_000, bytes_accessed=6_000_000, transcendentals=0),
        name=kernel.__name__,
    )(*args)


def to_everyone(x, axes, peers, groups=None):
    copies = jnp.broadcast_to(x[None], (peers, *x.shape)).reshape(-1, x.shape[-1])
    return lax.all_to_all(copies, axes, 0, 0, tiled=True, axis_index_groups=groups)


def swap(x):
    return lax.ppermute(x, "ao", [(0, 1), (1, 0)])


def body(cholesky, coefficients):
    shard = jnp.pad(coefficients, ((0, 0), (0, SHARD_PAD - SHARD)))
    line = to_everyone(shard, "vec_2", LINE)
    plane = ("vec_0", "vec_1", "ao")
    raw = to_everyone(line.reshape(LINE_ROWS, LANES), plane, 4, plane_groups(False))
    raw = to_everyone(raw.reshape(4 * LINE_ROWS, LANES), plane, 4, plane_groups(True))
    raw = raw.reshape(128 * SHARD_ROWS, LANES)
    half = jax.ShapeDtypeStruct((NOCC, HALF_PAD), F32)
    stacked = jax.ShapeDtypeStruct((2 * NOCC, HALF_PAD), BF16)
    table_like = jax.ShapeDtypeStruct((HALF_BLOCKS * PITCH, LANES), F32)
    occupied = pltpu.VMEM((HALF_PAD, LANES), F32)
    both, send = call(occupied_kernel, (stacked, half), raw, cholesky, scratch=(occupied,))
    came = swap(send)
    table, keep = call(middle_kernel, (table_like, half), raw, cholesky, both)
    both, send = call(leaving_kernel, (stacked, half), keep, came, table)
    came = swap(send)
    own_table = pltpu.VMEM(table_like.shape, F32)
    (keep,) = call(staying_kernel, (half,), raw, both, scratch=(own_table,))
    mine = keep + came
    owned = lax.all_to_all(mine, VEC, 0, 0, tiled=True)
    return owned[:, None, :HALF_VIR]


def solution(mesh):
    split_mesh = Mesh(mesh.devices.reshape(4, 4, 8, mesh.shape["ao"]), (*VEC, "ao"))
    in_specs = (P(VEC, "ao", None), P("ao", VEC))
    out_specs = P(None, VEC, "ao")
    return jax.shard_map(body, mesh=split_mesh, in_specs=in_specs, out_specs=out_specs, check_vma=False)
```

time: 90.1 us -> 88.6 us (0.983)
  waiting for transfers between devices: 1.81 us -> 0.01 us
    ppermute x2, waiting for transfers between devices: 1.81 us -> 0.01 us  [swap(): return lax.ppermute(x, 'ao', [(0, 1), (1, 0)])]
    pallas_call x3 -> x4, Pallas kernels: 5.56 us -> 6.01 us  [call(): pl.pallas_call(kernel, out_shape=outs, in_specs=[VMEM] * len(args), out_s...]
  transfers between devices with their start and end apart: 2 -> 2, of which waited for: 2 -> 0; matrix products, arithmetic and copies ran while one was open for 0% -> 0% of each run, Pallas kernels for 1% -> 5%
where the time goes in v4:
time: 88.6 us; the launch traced here: 88.4 us
  blocking collectives  74.1 us (84%)
  Pallas kernels  6.01 us (7%)
  starting transfers between devices  5.76 us (7%)
  local copies, waits for them, and re-layouts  2.36 us (3%)
    all_to_all x3, blocking collectives, to_everyone(): lax.all_to_all(copies, axes, 0, 0, tiled=True, axis_index_groups=groups)  53.1 us
    all_to_all x1, blocking collectives, body(): owned = lax.all_to_all(mine, VEC, 0, 0, tiled=True)  21 us
    pallas_call x4, Pallas kernels, call(): pl.pallas_call(kernel, out_shape=outs, in_specs=[VMEM] * len(args), out_s...  6.01 us
    ppermute x2, starting transfers between devices, swap(): return lax.ppermute(x, 'ao', [(0, 1), (1, 0)])  5.76 us
  transfers between devices with their start and end apart: 2, of which 0 were waited for; matrix products, arithmetic and copies ran while one was open for 0% of the time, Pallas kernels for 5%

profile of v4, /device:TPU:1, one launch (start us, length us, event | category | flops | bytes accessed | tf_op | source)
XLA Modules:
  0.0 88.4 jit_solution(15350035741944984310)
XLA Ops:
  0.0 0.8 pad_reduce_fusion
  0.8 0.1 reshape.26
  0.9 17.5 %all_to_all.32 = f32[8,1,5632]{2,1,0:T(1,128)S(1)} all-to-all(f32[8,1,5632]{2,1,0:T(1,128)S(1)} %reshape.26), channel_id=1, replica_groups=mesh['vec_0'=4,'vec_1'=4,'vec_2'=8,'ao'=2] {'vec_2'}, dimensions={0} | all-to-all | bytes 360448 | tf_op jit(solution)/shard_map/all_to_all | solution.py:202
  18.4 12.1 %all_to_all.33 = f32[4,352,128]{2,1,0:T(8,128)S(1)} all-to-all(f32[4,352,128]{2,1,0:T(8,128)S(1)} %broadcast_in_dim.11), channel_id=1, replica_groups={{0,64,128,192},{16,80,144,208},{32,96,160,224},{48,112,176,240},{1,17,3..., dimensions={0} | all-to-all | bytes 1441792 | tf_op jit(solution)/shard_map/all_to_all | solution.py:202
  30.5 0.2 broadcast_in_dim.25
  30.7 0.0 copy-start
  30.7 23.5 %all_to_all.34 = f32[4,1408,128]{2,1,0:T(8,128)S(1)} all-to-all(f32[4,1408,128]{2,1,0:T(8,128)S(1)} %broadcast_in_dim.25), channel_id=1, replica_groups={{0,16,32,48},{64,80,96,112},{128,144,160,176},{192,208,224,240},{1,65,1..., dimensions={0} | all-to-all | bytes 5767168 | tf_op jit(solution)/shard_map/all_to_all | solution.py:202
  54.2 0.0 copy-done
  54.2 1.3 %occupied_kernel.1 = (bf16[256,640]{1,0:T(8,128)(2,1)S(1)}, f32[128,640]{1,0:T(8,128)S(1)}) custom-call(f32[5632,128]{1,0:T(8,128)S(1)} %bitcast.10, f32[1,600,1200]{2,1,0:T(8,128)S(1)} %copy-done), custom_call_target="tpu_custom_call" | custom-call | flops 600000000 | bytes 6000000 | tf_op jit(solution)/shard_map/occupied_kernel/pallas_call | solution.py:188
  55.5 5.7 %collective-permute-start = (f32[128,640]{1,0:T(8,128)S(1)}, f32[128,640]{1,0:T(8,128)S(1)}, u32[]{:S(2)}, u32[]{:S(2)}) collective-permute-start(f32[128,640]{1,0:T(8,128)S(1)} %get-tuple-element.13), channel_id=1, source_target_pairs={{0,1},{1,0},{2,3},{3,2},{4,5},{5,4},{6,7},{7,6},{8,9},{9,8},{10,11... | collective-permute-start | bytes 983048 | tf_op jit(solution)/shard_map/ppermute | solution.py:206
  61.2 2.2 %middle_kernel.1 = (f32[3205,128]{1,0:T(8,128)S(1)}, f32[128,640]{1,0:T(8,128)S(1)}) custom-call(f32[5632,128]{1,0:T(8,128)S(1)} %bitcast.11, f32[1,600,1200]{2,1,0:T(8,128)S(1)} %copy-done, bf16[256,640]{1,0:T(8,128)(2,1)S(1)} %get-tuple-element.11.both), custom_call_target="tpu_custom_call" | custom-call | flops 600000000 | bytes 6000000 | tf_op jit(solution)/shard_map/middle_kernel/pallas_call | solution.py:188
  63.4 0.0 collective-permute-done.came
  63.4 0.6 leaving_kernel.1
  64.0 0.1 collective-permute-start.1
  64.1 1.9 %staying_kernel.1 = f32[128,640]{1,0:T(8,128)S(1)} custom-call(f32[5632,128]{1,0:T(8,128)S(1)} %bitcast.12, bf16[256,640]{1,0:T(8,128)(2,1)S(1)} %get-tuple-element.15.both), custom_call_target="tpu_custom_call" | custom-call | flops 600000000 | bytes 6000000 | tf_op jit(solution)/shard_map/staying_kernel/pallas_call | solution.py:188
  66.0 0.0 collective-permute-done.1
  66.1 0.3 copy.4
  66.4 21.0 %all_to_all.35 = f32[128,1,640]{2,1,0:T(1,128)S(1)} all-to-all(f32[128,1,640]{2,1,0:T(1,128)S(1)} %copy.4), channel_id=1, replica_groups=mesh['vec_0'=4,'vec_1'=4,'vec_2'=8,'ao'=2] {'vec_0','vec_1','vec_2'}, dimensions={0} | all-to-all | bytes 655360 | tf_op jit(solution)/shard_map/all_to_all | solution.py:228
  87.5 0.8 copy.5
  (4 shorter events, 0.1 us)
Async XLA Ops:
  30.7 23.5 %copy-start = (f32[1,600,1200]{2,1,0:T(8,128)S(1)}, f32[1,600,1200]{2,1,0:T(8,128)}, u32[]{:S(2)}) copy-start(f32[1,600,1200]{2,1,0:T(8,128)} %chol.3) | copy-start | bytes 8640004
  55.5 7.9 %collective-permute-start = (f32[128,640]{1,0:T(8,128)S(1)}, f32[128,640]{1,0:T(8,128)S(1)}, u32[]{:S(2)}, u32[]{:S(2)}) collective-permute-start(f32[128,640]{1,0:T(8,128)S(1)} %get-tuple-element.13), channel_id=1, source_target_pairs={{0,1},{1,0},{2,3},{3,2},{4,5},{5,4},{6,7},{7,6},{8,9},{9,8},{10,11... | collective-permute-start | bytes 983048 | tf_op jit(solution)/shard_map/ppermute | solution.py:206
  64.0 2.0 %collective-permute-start.1 = (f32[128,640]{1,0:T(8,128)S(1)}, f32[128,640]{1,0:T(8,128)S(1)}, u32[]{:S(2)}, u32[]{:S(2)}) collective-permute-start(f32[128,640]{1,0:T(8,128)S(1)} %get-tuple-element.16), channel_id=1, source_target_pairs={{0,1},{1,0},{2,3},{3,2},{4,5},{5,4},{6,7},{7,6},{8,9},{9,8},{10,11... | collective-permute-start | bytes 983048 | tf_op jit(solution)/shard_map/ppermute | solution.py:206

commit v5 on v4

--- a/solution.py
+++ b/solution.py
@@ -43,12 +43,6 @@
     return hi, (x - hi.astype(F32)).astype(BF16)
 
 
-def padded_half(chol, h):
-    part = chol[0, :, h * HALF : (h + 1) * HALF]
-    part = jnp.concatenate([part, jnp.zeros((HALF, HALF_PAD - HALF), F32)], axis=1)
-    return jnp.concatenate([part, jnp.zeros((HALF_PAD - HALF, HALF_PAD), F32)], axis=0)
-
-
 def each_row(raw, column, columns, store):
     own = lax.axis_index("ao")
     lane = lax.broadcasted_iota(jnp.int32, (8, LANES), 1)
@@ -83,7 +77,7 @@
             store(g * GROUP_ROWS + r, value)
         return carry
 
-    lax.fori_loop(0, 8, group, 0)
+    lax.fori_loop(0, 8, group, 0, unroll=4)
 
 
 def three_products(both, hi, lo):
@@ -101,7 +95,15 @@
 
 
 def first_half(both, chol, h):
-    return three_products(both, *hi_lo(padded_half(chol, h)))
+    first = h * HALF // LANES * LANES
+    end = min(h * HALF + HALF_PAD, NAO)
+    part = chol[0, :, first:end]
+    rest = -(end - first) % LANES
+    if rest:
+        part = jnp.concatenate([part, jnp.zeros((HALF, rest), F32)], axis=1)
+    part = jnp.concatenate([part, jnp.zeros((HALF_PAD - HALF, part.shape[1]), F32)], axis=0)
+    skip = h * HALF - first
+    return three_products(both, *hi_lo(part))[:, skip : skip + HALF_PAD]
 
 
 def occupied_rows(raw, occupied, core):
@@ -168,6 +170,11 @@
     return three_products(both, *hi_lo(jnp.concatenate(blocks, axis=1)))
 
 
+def store_lines(out, value):
+    for j in range(HALF_BLOCKS):
+        out[pl.ds(j, NOCC, stride=HALF_BLOCKS), :] = value[:, j * LANES : (j + 1) * LANES]
+
+
 def middle_kernel(raw, chol, both, table, keep):
     virtual_rows(raw, table, False)
     for_half(True, keep, lambda h: first_half(both[...], chol, h))
@@ -176,12 +183,12 @@
 def leaving_kernel(kept, came, table, both_out, send):
     both = jnp.concatenate(hi_lo(kept[...] + came[...]), axis=0)
     both_out[...] = both
-    send[...] = second_half(both, table)
+    store_lines(send, second_half(both, table))
 
 
 def staying_kernel(raw, both, keep, table):
     virtual_rows(raw, table, True)
-    keep[...] = second_half(both[...], table)
+    store_lines(keep, second_half(both[...], table))
 
 
 def call(kernel, outs, *args, scratch=(), mib=16):
@@ -220,11 +227,12 @@
     both, send = call(occupied_kernel, (stacked, half), raw, cholesky, scratch=(occupied,))
     came = swap(send)
     table, keep = call(middle_kernel, (table_like, half), raw, cholesky, both)
-    both, send = call(leaving_kernel, (stacked, half), keep, came, table)
+    lines = jax.ShapeDtypeStruct((NOCC * HALF_BLOCKS, LANES), F32)
+    both, send = call(leaving_kernel, (stacked, lines), keep, came, table)
     came = swap(send)
     own_table = pltpu.VMEM(table_like.shape, F32)
-    (keep,) = call(staying_kernel, (half,), raw, both, scratch=(own_table,))
-    mine = keep + came
+    (keep,) = call(staying_kernel, (lines,), raw, both, scratch=(own_table,))
+    mine = (keep + came).reshape(NOCC, HALF_PAD)
     owned = lax.all_to_all(mine, VEC, 0, 0, tiled=True)
     return owned[:, None, :HALF_VIR]
 

time: 88.6 us -> 87.3 us (0.985)
  Pallas kernels: 6.01 us -> 4.97 us
    pallas_call x4, Pallas kernels: 6.01 us -> 4.97 us  [call(): pl.pallas_call(kernel, out_shape=outs, in_specs=[VMEM] * len(args), out_s...]
  transfers between devices with their start and end apart: 2 -> 2, of which waited for: 0 -> 1; matrix products, arithmetic and copies ran while one was open for 0% -> 0% of each run, Pallas kernels for 5% -> 4%
where the time goes in v5:
time: 87.3 us; the launch traced here: 87 us
  blocking collectives  74.2 us (85%)
  starting transfers between devices  5.58 us (6%)
  Pallas kernels  4.97 us (6%)
  local copies, waits for them, and re-layouts  2.02 us (2%)
    all_to_all x3, blocking collectives, to_everyone(): lax.all_to_all(copies, axes, 0, 0, tiled=True, axis_index_groups=groups)  53.1 us
    all_to_all x1, blocking collectives, body(): owned = lax.all_to_all(mine, VEC, 0, 0, tiled=True)  21.1 us
    ppermute x2, starting transfers between devices, swap(): return lax.ppermute(x, 'ao', [(0, 1), (1, 0)])  5.58 us
    pallas_call x4, Pallas kernels, call(): pl.pallas_call(kernel, out_shape=outs, in_specs=[VMEM] * len(args), out_s...  4.97 us
  transfers between devices with their start and end apart: 2, of which 1 were waited for; matrix products, arithmetic and copies ran while one was open for 0% of the time, Pallas kernels for 4%

profile of v5, /device:TPU:1, one launch (start us, length us, event | category | flops | bytes accessed | tf_op | source)
XLA Modules:
  0.0 87.0 jit_solution(2459331797453637121)
XLA Ops:
  0.0 0.8 pad_reduce_fusion
  0.8 0.1 reshape.28
  0.9 17.5 %all_to_all.32 = f32[8,1,5632]{2,1,0:T(1,128)S(1)} all-to-all(f32[8,1,5632]{2,1,0:T(1,128)S(1)} %reshape.28), channel_id=1, replica_groups=mesh['vec_0'=4,'vec_1'=4,'vec_2'=8,'ao'=2] {'vec_2'}, dimensions={0} | all-to-all | bytes 360448 | tf_op jit(solution)/shard_map/all_to_all | solution.py:209
  18.4 12.1 %all_to_all.33 = f32[4,352,128]{2,1,0:T(8,128)S(1)} all-to-all(f32[4,352,128]{2,1,0:T(8,128)S(1)} %broadcast_in_dim.11), channel_id=1, replica_groups={{0,64,128,192},{16,80,144,208},{32,96,160,224},{48,112,176,240},{1,17,3..., dimensions={0} | all-to-all | bytes 1441792 | tf_op jit(solution)/shard_map/all_to_all | solution.py:209
  30.5 0.2 broadcast_in_dim.25
  30.7 0.0 copy-start
  30.7 23.5 %all_to_all.34 = f32[4,1408,128]{2,1,0:T(8,128)S(1)} all-to-all(f32[4,1408,128]{2,1,0:T(8,128)S(1)} %broadcast_in_dim.25), channel_id=1, replica_groups={{0,16,32,48},{64,80,96,112},{128,144,160,176},{192,208,224,240},{1,65,1..., dimensions={0} | all-to-all | bytes 5767168 | tf_op jit(solution)/shard_map/all_to_all | solution.py:209
  54.2 0.0 copy-done
  54.2 1.3 %occupied_kernel.1 = (bf16[256,640]{1,0:T(8,128)(2,1)S(1)}, f32[128,640]{1,0:T(8,128)S(1)}) custom-call(f32[5632,128]{1,0:T(8,128)S(1)} %bitcast.9, f32[1,600,1200]{2,1,0:T(8,128)S(1)} %copy-done), custom_call_target="tpu_custom_call" | custom-call | flops 600000000 | bytes 6000000 | tf_op jit(solution)/shard_map/occupied_kernel/pallas_call | solution.py:195
  55.5 5.5 %collective-permute-start = (f32[128,640]{1,0:T(8,128)S(1)}, f32[128,640]{1,0:T(8,128)S(1)}, u32[]{:S(2)}, u32[]{:S(2)}) collective-permute-start(f32[128,640]{1,0:T(8,128)S(1)} %get-tuple-element.13), channel_id=1, source_target_pairs={{0,1},{1,0},{2,3},{3,2},{4,5},{5,4},{6,7},{7,6},{8,9},{9,8},{10,11... | collective-permute-start | bytes 983048 | tf_op jit(solution)/shard_map/ppermute | solution.py:213
  61.0 1.6 %middle_kernel.1 = (f32[3205,128]{1,0:T(8,128)S(1)}, f32[128,640]{1,0:T(8,128)S(1)}) custom-call(f32[5632,128]{1,0:T(8,128)S(1)} %bitcast.10, f32[1,600,1200]{2,1,0:T(8,128)S(1)} %copy-done, bf16[256,640]{1,0:T(8,128)(2,1)S(1)} %get-tuple-element.11.both), custom_call_target="tpu_custom_call" | custom-call | flops 600000000 | bytes 6000000 | tf_op jit(solution)/shard_map/middle_kernel/pallas_call | solution.py:195
  62.6 0.0 collective-permute-done.came
  62.6 0.6 leaving_kernel.1
  63.3 0.1 collective-permute-start.1
  63.4 1.5 %staying_kernel.1 = f32[640,128]{1,0:T(8,128)S(1)} custom-call(f32[5632,128]{1,0:T(8,128)S(1)} %bitcast.11, bf16[256,640]{1,0:T(8,128)(2,1)S(1)} %get-tuple-element.15.both), custom_call_target="tpu_custom_call" | custom-call | flops 600000000 | bytes 6000000 | tf_op jit(solution)/shard_map/staying_kernel/pallas_call | solution.py:195
  64.8 0.1 collective-permute-done.1
  65.0 21.1 %all_to_all.35 = f32[128,1,640]{2,1,0:T(1,128)S(1)} all-to-all(f32[128,1,640]{2,1,0:T(1,128)S(1)} %bitcast.14), channel_id=1, replica_groups=mesh['vec_0'=4,'vec_1'=4,'vec_2'=8,'ao'=2] {'vec_0','vec_1','vec_2'}, dimensions={0} | all-to-all | bytes 655360 | tf_op jit(solution)/shard_map/all_to_all | solution.py:236
  86.2 0.8 copy.5
  (4 shorter events, 0.1 us)
Async XLA Ops:
  30.7 23.5 %copy-start = (f32[1,600,1200]{2,1,0:T(8,128)S(1)}, f32[1,600,1200]{2,1,0:T(8,128)}, u32[]{:S(2)}) copy-start(f32[1,600,1200]{2,1,0:T(8,128)} %chol.3) | copy-start | bytes 8640004
  55.5 7.1 %collective-permute-start = (f32[128,640]{1,0:T(8,128)S(1)}, f32[128,640]{1,0:T(8,128)S(1)}, u32[]{:S(2)}, u32[]{:S(2)}) collective-permute-start(f32[128,640]{1,0:T(8,128)S(1)} %get-tuple-element.13), channel_id=1, source_target_pairs={{0,1},{1,0},{2,3},{3,2},{4,5},{5,4},{6,7},{7,6},{8,9},{9,8},{10,11... | collective-permute-start | bytes 983048 | tf_op jit(solution)/shard_map/ppermute | solution.py:213
  63.3 1.7 %collective-permute-start.1 = (f32[640,128]{1,0:T(8,128)S(1)}, f32[640,128]{1,0:T(8,128)S(1)}, u32[]{:S(2)}, u32[]{:S(2)}) collective-permute-start(f32[640,128]{1,0:T(8,128)S(1)} %get-tuple-element.16), channel_id=1, source_target_pairs={{0,1},{1,0},{2,3},{3,2},{4,5},{5,4},{6,7},{7,6},{8,9},{9,8},{10,11... | collective-permute-start | bytes 983048 | tf_op jit(solution)/shard_map/ppermute | solution.py:213
